TPU v7x, 32 devices: a whole 2x2x4 slice. The times are simulated.
32 devices in a mesh: role: 2 (over core), dev: 16 (over z, y, x).
Axes of the slice: x: 2, y: 2, z: 4, core: 2. Of those that a mesh axis runs over, the one named last changes fastest.
Arguments:
- table_rows: bfloat16 [32, 2048, 128], P('dev'), may hold values from -6 to 6
- piece_table: int32 [32], replicated, may hold values from 0 to 25, as said below
- bag_rows: int32 [32, 8192], P('dev'), may hold values from 0 to 2047
- bag_of: int32 [32, 8192], P('dev'), may hold values from 0 to 4095, never falling along the last dimension, each value on 1 to 8 neighbouring positions
- bag_weight: bfloat16 [32, 8192], P('dev'), may hold values from 0.25 to 2
- dense_input: bfloat16 [4096, 128], P('dev'), may hold values from -6 to 6
- labels: float32 [4096], P('dev'), may hold values from 0 to 1
- cross_u: bfloat16 [3456, 512], replicated, may hold values from -0.109375 to 0.109375
- cross_v: bfloat16 [512, 3456], replicated, may hold values from -0.25 to 0.25
- cross_bias: float32 [3456], replicated, may hold values from -3 to 3
- top_w1: bfloat16 [3456, 1024], replicated, may hold values from -0.109375 to 0.109375
- top_b1: float32 [1024], replicated, may hold values from -3 to 3
- out_w: bfloat16 [1024], replicated, may hold values from -0.375 to 0.375
Outputs:
- piece_grads: bfloat16 [16, 256, 32, 128], P(None, 'role', 'dev')
Inputs may be any that keep to these rules, and one draw needn't show every extreme that they name: `piece_table`: every one of the 26 tables owns one piece or more. `bag_of`: in each piece the bag numbers never fall along the lookups, and every sample has 1 to 8 lookups in every piece.
All inputs are finite; a program needn't handle non-finite values.
Results may differ from a plain program's by a relative error of at most 0.012.
The roundings to bfloat16 on the way count: a program that leaves them out, or rounds other values in their place, can miss the bound.
Values may be sent and summed in bfloat16 or wider, within the bound.
A program may use at most 128 MiB of HBM per device.

v0:
```python
import jax
import jax.numpy as jnp
from jax import lax
from jax.experimental import pallas as pl
from jax.experimental.pallas import tpu as pltpu
from jax.sharding import PartitionSpec as P

LANES = 128
WINDOW = 384
LOW = 256
CHUNKS = 2
NT = (((1,), (1,)), ((), ()))
NN = (((1,), (0,)), ((), ()))


def dot(a, b, dims=NN):
    return lax.dot_general(a, b, dims, preferred_element_type=jnp.float32)


def pool_kernel(
    owner_ref, first_ref, last_ref, table_ref, rows_ref, bags_ref, scale_ref,
    out_ref, lead_ref, spare_ref, spare_owner_ref, flipped, scale_wide,
):
    blocks, pieces, half, width = out_ref.shape
    length = table_ref.shape[1]
    total = rows_ref.shape[1]
    groups = length // LOW
    role = lax.axis_index("role")

    @pl.loop(0, lead_ref.shape[0])
    def _(t):
        lead_ref[t] = -1

    @pl.loop(0, spare_ref.shape[0])
    def _(e):
        spare_ref[e] = 0
        spare_owner_ref[e] = -1

    def assign(p, used):
        t = owner_ref[p]
        again = lead_ref[t] >= 0

        @pl.when(again)
        def _():
            spare_ref[used] = p
            spare_owner_ref[used] = t

        @pl.when(jnp.logical_not(again))
        def _():
            lead_ref[t] = p

        return used + again.astype(jnp.int32)

    lax.fori_loop(0, owner_ref.shape[0], assign, jnp.int32(0))
    scale_wide[...] = scale_ref[...].astype(jnp.float32)
    for p in range(pieces):
        for g in range(groups):
            flipped[p, g * width : (g + 1) * width, :] = (
                table_ref[p, g * LOW : (g + 1) * LOW, :].astype(jnp.float32).T.astype(jnp.bfloat16)
            )
    low_ids = lax.broadcasted_iota(jnp.int32, (LOW, WINDOW), 0)
    bag_ids = lax.broadcasted_iota(jnp.int32, (half, WINDOW), 0)
    places = lax.broadcasted_iota(jnp.int32, (1, WINDOW), 1)

    def window(p, base, begin, first_bag):
        start = pl.multiple_of(jnp.minimum(begin, total - WINDOW), LANES)
        span = pl.ds(start, WINDOW)
        ids = rows_ref[pl.ds(p, 1), span]
        bags = bags_ref[pl.ds(p, 1), span] - first_bag
        bags = jnp.where(places + start >= begin, bags, -1)
        scale = scale_wide[pl.ds(p, 1), span]
        low, high = ids % LOW, ids // LOW
        hot = jnp.where(low_ids == low, 1.0, 0.0).astype(jnp.bfloat16)
        picked = dot(flipped[p, :width, :], hot)
        for g in range(1, groups):
            picked = jnp.where(high == g, dot(flipped[p, g * width : (g + 1) * width, :], hot), picked)
        spread = jnp.where(bag_ids == bags, scale, 0.0).astype(jnp.bfloat16)
        return dot(spread, picked.astype(jnp.bfloat16), NT)

    @pl.loop(0, blocks)
    def _(k):
        first_bag = (2 * k + role) * half
        bases = [first_ref[p, k] // LANES * LANES for p in range(pieces)]
        sums = [window(p, bases[p], bases[p], first_bag) for p in range(pieces)]
        for p in range(pieces):
            out_ref[k, p] = sums[p].astype(jnp.bfloat16)
        for p in range(pieces):
            count = (last_ref[p, k] - bases[p] + WINDOW - 1) // WINDOW

            @pl.when(count > 1)
            def _():
                def more(j, acc):
                    return acc + window(p, bases[p], bases[p] + j * WINDOW, first_bag)

                first = window(p, bases[p], bases[p], first_bag)
                out_ref[k, p] = lax.fori_loop(1, count, more, first).astype(jnp.bfloat16)


def pool(piece_table, table_rows, bag_rows, bag_of, bag_weight, half, blocks, tables):
    pieces, length, width = table_rows.shape
    role = lax.axis_index("role")
    edges = (2 * jnp.arange(blocks, dtype=jnp.int32) + role) * half
    first = jnp.sum((bag_of[:, None, :] < edges[None, :, None]).astype(jnp.int32), axis=2)
    last = jnp.sum((bag_of[:, None, :] < edges[None, :, None] + half).astype(jnp.int32), axis=2)
    spares = max(1, piece_table.shape[0] - tables)
    vmem = pl.BlockSpec(memory_space=pltpu.VMEM)
    smem = pl.BlockSpec(memory_space=pltpu.SMEM)
    return pl.pallas_call(
        pool_kernel,
        out_shape=[
            jax.ShapeDtypeStruct((blocks, pieces, half, width), jnp.bfloat16),
            jax.ShapeDtypeStruct((tables,), jnp.int32),
            jax.ShapeDtypeStruct((spares,), jnp.int32),
            jax.ShapeDtypeStruct((spares,), jnp.int32),
        ],
        in_specs=[smem, smem, smem, vmem, vmem, vmem, vmem],
        out_specs=[vmem, smem, smem, smem],
        scratch_shapes=[
            pltpu.VMEM((pieces, length // LOW * width, LOW), jnp.bfloat16),
            pltpu.VMEM(bag_weight.shape, jnp.float32),
        ],
        compiler_params=pltpu.CompilerParams(vmem_limit_bytes=40 * 1024 * 1024),
    )(piece_table, first, last, table_rows, bag_rows, bag_of, bag_weight)


def dense_kernel(
    owner_ref, lead_ref, spare_ref, spare_owner_ref, pooled_ref, dense_ref, label_ref, bias_ref, b1_ref,
    out_w_ref, u_hbm, v_hbm, w_hbm, out_ref,
    u_ref, v_ref, w_ref, feats, crossed, mixed_grad, grads, arrived, outgoing,
    sems, there_send, there_recv, back_send, back_recv,
):
    devices, local_pieces, half, width = pooled_ref.shape
    pieces = devices * local_pieces
    rows, wide = feats.shape
    tables = wide // width - 1
    role = lax.axis_index("role")
    me = lax.axis_index("dev")
    load_u = pltpu.make_async_copy(u_hbm, u_ref, sems.at[0])
    load_v = pltpu.make_async_copy(v_hbm, v_ref, sems.at[1])
    load_w = pltpu.make_async_copy(w_hbm, w_ref, sems.at[2])

    barrier = pltpu.get_barrier_semaphore()

    @pl.loop(1, devices)
    def _(s):
        pl.semaphore_signal(
            barrier, inc=1, device_id={"dev": (me + s) % devices}, device_id_type=pl.DeviceIdType.MESH
        )

    load_u.start()
    load_v.start()
    load_w.start()
    pl.semaphore_wait(barrier, devices - 1)

    def there(c, s):
        peer = (me + s) % devices
        return pltpu.make_async_remote_copy(
            src_ref=pooled_ref.at[peer, :, c * rows : (c + 1) * rows, :],
            dst_ref=arrived[c].at[me],
            send_sem=there_send.at[c, s],
            recv_sem=there_recv.at[c, s],
            device_id={"dev": peer},
            device_id_type=pl.DeviceIdType.MESH,
        )

    def back(c, s):
        peer = (me + s) % devices
        return pltpu.make_async_remote_copy(
            src_ref=outgoing[c].at[peer],
            dst_ref=out_ref.at[me, :, c * rows : (c + 1) * rows, :],
            send_sem=back_send.at[c, s],
            recv_sem=back_recv.at[c, s],
            device_id={"dev": peer},
            device_id_type=pl.DeviceIdType.MESH,
        )

    for c in range(CHUNKS):

        @pl.loop(1, devices)
        def _(s):
            there(c, s).start()

    for c in range(CHUNKS):
        arrived[c][me] = pooled_ref[me, :, c * rows : (c + 1) * rows, :]

    step = next(n for n in (3 * width, width) if wide % n == 0)
    parts = [slice(i, i + step) for i in range(0, wide, step)]
    out_weight = out_w_ref[...].astype(jnp.float32)[None, :]
    row_at = lax.broadcasted_iota(jnp.int32, (rows, 2 * half), 0)
    column_at = lax.broadcasted_iota(jnp.int32, (rows, 2 * half), 1)
    spares = pieces - tables

    for c in range(CHUNKS):
        feats[:, :width] = dense_ref[pl.ds(pl.multiple_of(role * half + c * rows, rows), rows), :].astype(jnp.float32)

        @pl.loop(1, devices)
        def _(s):
            there(c, s).wait_recv()

        def piece(index):
            return arrived[c][index // local_pieces, index % local_pieces].astype(jnp.float32)

        @pl.loop(0, tables)
        def _(t):
            def add(e, acc):
                return acc + piece(spare_ref[e]) * jnp.where(spare_owner_ref[e] == t, 1.0, 0.0)

            acc = piece(lead_ref[t])
            if spares <= 16:
                for e in range(spares):
                    acc = add(e, acc)
            else:
                acc = lax.fori_loop(0, spares, add, acc)
            feats[:, pl.ds(pl.multiple_of((t + 1) * width, width), width)] = acc

        if c == 0:
            load_u.wait()
        low_rank = dot(feats[...].astype(jnp.bfloat16), u_ref[...]).astype(jnp.bfloat16)
        if c == 0:
            load_v.wait()
            load_w.wait()
        pre_act = b1_ref[...][None, :]
        for part in parts:
            cross_out = dot(low_rank, v_ref[:, part]) + bias_ref[part][None, :]
            crossed[:, part] = cross_out
            own = feats[:, part]
            pre_act = pre_act + dot((own * cross_out + own).astype(jnp.bfloat16), w_ref[part, :])
        sig_act = jax.nn.sigmoid(pre_act)
        logits = jnp.sum(pre_act * sig_act * out_weight, axis=1, keepdims=True)
        labels = jnp.sum(
            jnp.where(row_at + (role * half + c * rows) == column_at, label_ref[...][None, :], 0.0),
            axis=1,
            keepdims=True,
        )
        grad_logit = jax.nn.sigmoid(logits) - labels
        slope = sig_act * (1.0 + pre_act * (1.0 - sig_act))
        grad_act = (grad_logit * out_weight * slope).astype(jnp.bfloat16)
        grad_low = jnp.zeros((rows, u_ref.shape[1]), jnp.float32)
        for part in parts:
            grad_mixed = dot(grad_act, w_ref[part, :], NT)
            grad_cross = (grad_mixed * feats[:, part]).astype(jnp.bfloat16)
            mixed_grad[:, part] = grad_mixed * (crossed[:, part] + 1.0)
            grad_low = grad_low + dot(grad_cross, v_ref[:, part], NT)
        grad_low = grad_low.astype(jnp.bfloat16)
        for part in parts:
            total = (mixed_grad[:, part] + dot(grad_low, u_ref[part, :], NT)).astype(jnp.bfloat16)
            for i in range(step // width):
                grads[part.start // width + i] = total[:, i * width : (i + 1) * width]

        @pl.loop(0, devices)
        def _(d):
            for i in range(local_pieces):
                outgoing[c][d, i] = grads[owner_ref[d * local_pieces + i] + 1]

        @pl.loop(1, devices)
        def _(s):
            back(c, s).start()

        out_ref[me, :, c * rows : (c + 1) * rows, :] = outgoing[c][me]

    for c in range(CHUNKS):

        @pl.loop(1, devices)
        def _(s):
            there(c, s).wait_send()
            back(c, s).wait_send()
            back(c, s).wait_recv()


def dense(chosen, pooled, piece_table, dense_input, labels, cross_u, cross_v, cross_bias, top_w1, top_b1, out_w):
    devices, local_pieces, half, width = pooled.shape
    rows = half // CHUNKS
    wide = cross_u.shape[0]
    vmem = pl.BlockSpec(memory_space=pltpu.VMEM)
    smem = pl.BlockSpec(memory_space=pltpu.SMEM)
    anywhere = pl.BlockSpec(memory_space=pl.ANY)
    block = pltpu.VMEM((devices, local_pieces, rows, width), jnp.bfloat16)
    return pl.pallas_call(
        dense_kernel,
        out_shape=jax.ShapeDtypeStruct(pooled.shape, jnp.bfloat16),
        in_specs=[smem] * 4 + [vmem] * 6 + [anywhere] * 3,
        out_specs=vmem,
        scratch_shapes=[
            pltpu.VMEM(cross_u.shape, jnp.bfloat16),
            pltpu.VMEM(cross_v.shape, jnp.bfloat16),
            pltpu.VMEM(top_w1.shape, jnp.bfloat16),
            pltpu.VMEM((rows, wide), jnp.float32),
            pltpu.VMEM((rows, wide), jnp.float32),
            pltpu.VMEM((rows, wide), jnp.float32),
            pltpu.VMEM((wide // width, rows, width), jnp.bfloat16),
            [block] * CHUNKS,
            [block] * CHUNKS,
            pltpu.SemaphoreType.DMA((3,)),
        ]
        + [pltpu.SemaphoreType.DMA((CHUNKS, devices))] * 4,
        compiler_params=pltpu.CompilerParams(
            vmem_limit_bytes=56 * 1024 * 1024, collective_id=0, has_side_effects=True
        ),
    )(
        piece_table, *chosen, pooled, dense_input, labels, cross_bias,
        top_b1, out_w, cross_u, cross_v, top_w1,
    )


def local(
    table_rows, piece_table, bag_rows, bag_of, bag_weight, dense_input, labels,
    cross_u, cross_v, cross_bias, top_w1, top_b1, out_w,
):
    devices = lax.axis_size("dev")
    half = dense_input.shape[0] // 2
    tables = cross_bias.shape[0] // dense_input.shape[1] - 1
    pooled, *chosen = pool(piece_table, table_rows, bag_rows, bag_of, bag_weight, half, devices, tables)
    returned = dense(
        chosen, pooled, piece_table, dense_input, labels, cross_u, cross_v, cross_bias, top_w1, top_b1, out_w
    )
    return returned.transpose(0, 2, 1, 3)


def solution(mesh):
    split, whole = P("dev"), P()
    return jax.shard_map(
        local,
        mesh=mesh,
        in_specs=(split, whole, split, split, split, split, split) + (whole,) * 6,
        out_specs=P(None, "role", "dev", None),
        check_vma=False,
    )
```

profile of v0, /device:TPU:0, one launch (start us, length us, event | category | flops | bytes accessed | tf_op | source)
XLA Modules:
  0.0 94.8 jit_solution(2174885908895628423)
XLA Ops:
  0.0 1.3 %convert_reduce_fusion = (s32[2,16]{1,0:T(2,128)S(1)}, s32[2,16]{1,0:T(2,128)S(1)}) fusion(s32[2,8192]{1,0:T(2,128)} %bags_ref.1, s32[16]{0:T(128)S(1)} %get-tuple-element.16, s32[16]{0:T(128)S(1)} %get-tuple-element.15), kind=kLoop, calls=%fused_computation | loop fusion | flops 1572800 | bytes 65920 | tf_op jit(solution)/shard_map/reduce_sum | solution.py:104
  1.3 0.0 copy-start.1
  1.3 1.2 %copy-done.1 = bf16[2,2048,128]{2,1,0:T(8,128)(2,1)S(1)} copy-done((bf16[2,2048,128]{2,1,0:T(8,128)(2,1)S(1)}, bf16[2,2048,128]{2,1,0:T(8,128)(2,1)}, u32[]{:S(2)}) %copy-start.1) | copy-done | bytes 1048600
  2.5 0.0 copy-start.2
  2.5 0.8 copy-done.2
  3.3 0.0 copy-start.3
  3.3 0.8 copy-done.3
  4.2 0.0 copy-start.4
  4.2 0.8 copy-done.4
  4.9 0.0 copy-start.5
  4.9 0.7 copy-done.5
  5.6 21.8 %shard_map.127 = (bf16[16,2,128,128]{3,2,1,0:T(8,128)(2,1)S(1)}, s32[26]{0:T(128)S(1)}, s32[6]{0:T(128)S(1)}, s32[6]{0:T(128)S(1)}) custom-call(s32[32]{0:T(128)S(1)} %copy-done.5, s32[2,16]{1,0:T(2,128)S(1)} %get-tuple-element.14.first_ref, s32[2,16]{1,0:T(2,128)S(1)} %get-tuple-element.13.last_ref, bf16[2,2048,128]{2,1,0:T(8,128)(2,1)S(1)} %copy-done.1, ...), custom_call_target="tpu_custom_call" | custom-call | tf_op jit(solution)/shard_map/pallas_call | solution.py:108
  27.4 0.0 copy-start
  27.4 1.0 %copy-done = bf16[16,2,128,128]{3,2,1,0:T(8,128)(2,1)} copy-done((bf16[16,2,128,128]{3,2,1,0:T(8,128)(2,1)}, bf16[16,2,128,128]{3,2,1,0:T(8,128)(2,1)S(1)}, u32[]{:S(2)}) %copy-start) | copy-done | bytes 1048600
  28.4 0.0 copy-start.6
  28.4 0.5 copy-done.6
  28.9 0.0 copy-start.7
  28.9 0.6 copy-done.7
  29.5 0.0 copy-start.8
  29.5 0.5 copy-done.8
  30.0 61.5 %shard_map.128 = bf16[16,2,128,128]{3,2,1,0:T(8,128)(2,1)} custom-call(s32[32]{0:T(128)} %owner_ref.3, s32[26]{0:T(128)} %copy-done.6, s32[6]{0:T(128)} %copy-done.7, s32[6]{0:T(128)} %copy-done.8, bf16[16,2,128,128]{3,2,1,0:T(8,128)(2,1)} %copy-done, bf16[256,128]{1,0:T(8,128)(2,1)} %dense_ref.1, f32[256]{0:T(256)} %label_ref.1, f32[3456]{0:T(1024)} %bias_ref.1, ...), custom_call_target="tpu_custom_call" | custom-call | tf_op jit(solution)/shard_map/pallas_call | solution.py:278
  91.6 3.3 %copy.15 = bf16[16,128,2,128]{3,2,1,0:T(2,128)(2,1)} copy(bf16[16,128,2,128]{3,1,2,0:T(8,128)(2,1)} %bitcast.1) | data formatting | bytes 2097152 | tf_op jit(solution)/shard_map/transpose | solution.py:316
  (1 shorter events, 0.0 us)
Async XLA Ops:
  1.3 1.2 %copy-start.1 = (bf16[2,2048,128]{2,1,0:T(8,128)(2,1)S(1)}, bf16[2,2048,128]{2,1,0:T(8,128)(2,1)}, u32[]{:S(2)}) copy-start(bf16[2,2048,128]{2,1,0:T(8,128)(2,1)} %table_ref.1) | copy-start | bytes 3145732
  2.5 0.8 copy-start.2
  3.3 0.8 copy-start.3
  4.2 0.8 copy-start.4
  4.9 0.7 copy-start.5
  27.4 1.0 %copy-start = (bf16[16,2,128,128]{3,2,1,0:T(8,128)(2,1)}, bf16[16,2,128,128]{3,2,1,0:T(8,128)(2,1)S(1)}, u32[]{:S(2)}) copy-start(bf16[16,2,128,128]{3,2,1,0:T(8,128)(2,1)S(1)} %get-tuple-element.12.pooled_ref) | copy-start | bytes 3145732
  28.4 0.5 copy-start.6
  28.9 0.6 copy-start.7
  29.5 0.5 copy-start.8
where the time goes:
time: 93.5 us; the launch traced here: 94.8 us
  Pallas kernels  83.4 us (89%)
  local copies, waits for them, and re-layouts  10.2 us (11%)
  other arithmetic  1.26 us (1%)
    pallas_call x1, Pallas kernels, dense(): pl.pallas_call(dense_kernel, out_shape=jax.ShapeDtypeStruct(pooled.shape,...  61.5 us
    pallas_call x1, Pallas kernels, pool(): pl.pallas_call(pool_kernel, out_shape=[jax.ShapeDtypeStruct((blocks, piec...  21.8 us
    unnamed x18, local copies, waits for them, and re-layouts  6.9 us
    transpose x1, local copies, waits for them, and re-layouts, local(): return returned.transpose(0, 2, 1, 3)  3.28 us

commit v1 on v0

v1 whole, which is shorter than its diff:
```python
import functools

import jax
import jax.numpy as jnp
from jax import lax
from jax.experimental import pallas as pl
from jax.experimental.pallas import tpu as pltpu
from jax.sharding import PartitionSpec as P

LANES = 128
WINDOW = 2 * LANES
LOW = 256
CHUNKS = 2
NT = (((1,), (1,)), ((), ()))
NN = (((1,), (0,)), ((), ()))


def dot(a, b, dims=NN):
    return lax.dot_general(a, b, dims, preferred_element_type=jnp.float32)


def flip(tile):
    return tile.astype(jnp.float32).T.astype(jnp.bfloat16)


def pick(table, width, ids):
    low_ids = lax.broadcasted_iota(jnp.int32, (LOW, ids.shape[1]), 0)
    low, high = ids % LOW, ids // LOW
    hot = jnp.where(low_ids == low, 1.0, 0.0).astype(jnp.bfloat16)
    picked = dot(table[:width, :], hot)
    for g in range(1, table.shape[0] // width):
        picked = jnp.where(high == g, dot(table[g * width : (g + 1) * width, :], hot), picked)
    return picked.astype(jnp.bfloat16)


def spread_out(bags, scale, rows):
    bag_ids = lax.broadcasted_iota(jnp.int32, (rows, bags.shape[1]), 0)
    return jnp.where(bag_ids == bags, scale, 0.0).astype(jnp.bfloat16)


def plan_kernel(
    tables, owner_ref, bags_ref, rows_hbm, scale_hbm, table_hbm, plan_ref, base_ref, extra_hbm,
    rows_ref, scale_ref, scale_wide, table_ref, flipped, stage, sems,
):
    blocks, pieces, half, width = extra_hbm.shape
    tiles = bags_ref.shape[0]
    rows = half // CHUNKS
    shift = rows.bit_length() - 1
    spares = max(1, owner_ref.shape[0] - tables)
    flags = tables + 2 * spares
    role = lax.axis_index("role")

    @pl.loop(0, tables)
    def _(t):
        plan_ref[t] = -1

    @pl.loop(0, spares)
    def _(e):
        plan_ref[tables + e] = 0
        plan_ref[tables + spares + e] = -1

    def assign(p, used):
        t = owner_ref[p]
        again = plan_ref[t] >= 0

        @pl.when(again)
        def _():
            plan_ref[tables + used] = p
            plan_ref[tables + spares + used] = t

        @pl.when(jnp.logical_not(again))
        def _():
            plan_ref[t] = p

        return used + again.astype(jnp.int32)

    lax.fori_loop(0, owner_ref.shape[0], assign, jnp.int32(0))

    @pl.loop(0, plan_ref.shape[0] - flags)
    def _(i):
        plan_ref[flags + i] = 0

    group = lax.broadcasted_iota(jnp.int32, base_ref.shape, 1)
    edges = (2 * (group // CHUNKS) + role) * half + group % CHUNKS * rows

    ahead = WINDOW // LANES

    def count(t, state):
        base, over = state
        here = bags_ref[t]
        base = base + jnp.where(here[:, LANES - 1 :] < edges, 1, 0)
        same = (here >> shift) == (bags_ref[t + ahead] >> shift)
        return base, jnp.maximum(over, jnp.where(same, 1, 0))

    state = (jnp.zeros(base_ref.shape, jnp.int32), jnp.zeros((pieces, LANES), jnp.int32))
    base, over = lax.fori_loop(0, tiles - ahead, count, state, unroll=True if tiles <= 64 else 8)
    for t in range(tiles - ahead, tiles):
        base = base + jnp.where(bags_ref[t][:, LANES - 1 :] < edges, 1, 0)
    base_ref[...] = jnp.minimum(base, tiles - ahead - 1)

    @pl.when(jnp.max(over) > 0)
    def _():
        loads = [
            pltpu.make_async_copy(rows_hbm, rows_ref, sems.at[0]),
            pltpu.make_async_copy(scale_hbm, scale_ref, sems.at[1]),
            pltpu.make_async_copy(table_hbm, table_ref, sems.at[2]),
        ]
        for load in loads:
            load.start()
        for load in loads:
            load.wait()
        scale_wide[...] = scale_ref[...].astype(jnp.float32)
        for p in range(pieces):
            for g in range(table_ref.shape[1] // LOW):
                flipped[p, g * width : (g + 1) * width, :] = flip(table_ref[p, g * LOW : (g + 1) * LOW, :])

        for p in range(pieces):

            @pl.loop(0, blocks * CHUNKS)
            def _(e):
                k, c = e // CHUNKS, e % CHUNKS
                edge = (2 * k + role) * half + c * rows
                bags = bags_ref[:, p, :]
                first = jnp.sum(jnp.where(bags < edge, 1, 0))
                last = jnp.sum(jnp.where(bags < edge + rows, 1, 0))
                begin = first // LANES

                def more(t, acc):
                    picked = pick(flipped[p], width, rows_ref[t, p : p + 1, :])
                    spread = spread_out(bags_ref[t, p : p + 1, :] - edge, scale_wide[t, p : p + 1, :], rows)
                    return acc + dot(spread, picked, NT)

                @pl.when(last - first > WINDOW)
                def _():
                    plan_ref[flags + (k * pieces + p) * CHUNKS + c] = 1
                    end = (last + LANES - 1) // LANES
                    acc = lax.fori_loop(begin, end, more, jnp.zeros((rows, width), jnp.float32))
                    stage[...] = acc.astype(jnp.bfloat16)
                    put = pltpu.make_async_copy(
                        stage, extra_hbm.at[k, p, pl.ds(pl.multiple_of(c * rows, rows), rows), :], sems.at[0]
                    )
                    put.start()
                    put.wait()


def plan(piece_table, table_rows, bag_rows, bag_of, bag_weight, half, blocks, tables):
    pieces, length, width = table_rows.shape
    spares = max(1, piece_table.shape[0] - tables)
    lanes = -(-blocks * CHUNKS // LANES) * LANES
    vmem = pl.BlockSpec(memory_space=pltpu.VMEM)
    smem = pl.BlockSpec(memory_space=pltpu.SMEM)
    hbm = pl.BlockSpec(memory_space=pltpu.HBM)
    return pl.pallas_call(
        functools.partial(plan_kernel, tables),
        out_shape=[
            jax.ShapeDtypeStruct((tables + 2 * spares + blocks * pieces * CHUNKS,), jnp.int32),
            jax.ShapeDtypeStruct((pieces, lanes), jnp.int32),
            jax.ShapeDtypeStruct((blocks, pieces, half, width), jnp.bfloat16),
        ],
        in_specs=[smem, vmem, hbm, hbm, hbm],
        out_specs=[smem, vmem, hbm],
        scratch_shapes=[
            pltpu.VMEM(bag_rows.shape, jnp.int32),
            pltpu.VMEM(bag_weight.shape, jnp.bfloat16),
            pltpu.VMEM(bag_weight.shape, jnp.float32),
            pltpu.VMEM(table_rows.shape, jnp.bfloat16),
            pltpu.VMEM((pieces, length // LOW * width, LOW), jnp.bfloat16),
            pltpu.VMEM((half // CHUNKS, width), jnp.bfloat16),
            pltpu.SemaphoreType.DMA((3,)),
        ],
        compiler_params=pltpu.CompilerParams(vmem_limit_bytes=60 * 1024 * 1024),
    )(piece_table, bag_of, bag_rows, bag_weight, table_rows)


def step_kernel(
    plan_ref, base_ref, owner_ref, dense_ref, label_ref, bias_ref, b1_ref, out_w_ref,
    bags_hbm, rows_hbm, scale_hbm, table_hbm, extra_hbm, u_hbm, v_hbm, w_hbm, out_ref,
    bags_ref, rows_ref, scale_ref, scale_wide, table_ref, flipped, extra_ref, pooled,
    u_ref, v_ref, w_ref, feats, crossed, mixed_grad, grads, arrived, outgoing,
    sems, there_send, there_recv, back_send, back_recv,
):
    devices, local_pieces, half, width = out_ref.shape
    pieces = devices * local_pieces
    rows, wide = feats.shape
    tables = wide // width - 1
    spares = max(1, pieces - tables)
    flags = tables + 2 * spares
    role = lax.axis_index("role")
    me = lax.axis_index("dev")
    small = [
        pltpu.make_async_copy(bags_hbm, bags_ref, sems.at[0]),
        pltpu.make_async_copy(rows_hbm, rows_ref, sems.at[1]),
        pltpu.make_async_copy(scale_hbm, scale_ref, sems.at[2]),
        pltpu.make_async_copy(table_hbm, table_ref, sems.at[3]),
        pltpu.make_async_copy(extra_hbm, extra_ref, sems.at[4]),
    ]
    load_u = pltpu.make_async_copy(u_hbm, u_ref, sems.at[5])
    load_v = pltpu.make_async_copy(v_hbm, v_ref, sems.at[6])
    load_w = pltpu.make_async_copy(w_hbm, w_ref, sems.at[7])
    barrier = pltpu.get_barrier_semaphore()

    for load in small:
        load.start()

    @pl.loop(1, devices)
    def _(s):
        pl.semaphore_signal(
            barrier, inc=1, device_id={"dev": (me + s) % devices}, device_id_type=pl.DeviceIdType.MESH
        )

    load_u.start()
    load_v.start()
    load_w.start()

    def partner(s):
        if devices & (devices - 1):
            return (me + s) % devices
        peer = 0
        for b in range(devices.bit_length() - 1):
            bit = 1 << b
            peer = peer + bit * ((me // bit + s // bit) % 2)
        return peer

    def there(c, s):
        peer = partner(s)
        return pltpu.make_async_remote_copy(
            src_ref=pooled.at[peer, :, c * rows : (c + 1) * rows, :],
            dst_ref=arrived[c].at[me],
            send_sem=there_send.at[c, s],
            recv_sem=there_recv.at[c, s],
            device_id={"dev": peer},
            device_id_type=pl.DeviceIdType.MESH,
        )

    def back(c, s):
        peer = partner(s)
        return pltpu.make_async_remote_copy(
            src_ref=outgoing[c].at[peer],
            dst_ref=out_ref.at[me, :, c * rows : (c + 1) * rows, :],
            send_sem=back_send.at[c, s],
            recv_sem=back_recv.at[c, s],
            device_id={"dev": peer},
            device_id_type=pl.DeviceIdType.MESH,
        )

    for load in small:
        load.wait()
    scale_wide[...] = scale_ref[...].astype(jnp.float32)
    for p in range(local_pieces):
        for g in range(table_ref.shape[1] // LOW):
            flipped[p, g * width : (g + 1) * width, :] = flip(table_ref[p, g * LOW : (g + 1) * LOW, :])

    def window(k, p, c):
        edge = (2 * k + role) * half + c * rows
        at = base_ref[p, k * CHUNKS + c]

        def tiles(ref):
            return [ref[at + j, p : p + 1, :] for j in range(WINDOW // LANES + 1)]

        bags = tiles(bags_ref)
        early = bags[0] < edge

        def lay(parts):
            return jnp.concatenate([jnp.where(early, parts[-1], parts[0])] + parts[1:-1], axis=1)

        picked = pick(flipped[p], width, lay(tiles(rows_ref)))
        summed = dot(spread_out(lay(bags) - edge, lay(tiles(scale_wide)), rows), picked, NT)
        flag = jnp.zeros((rows, width), jnp.int32) + plan_ref[flags + (k * local_pieces + p) * CHUNKS + c]
        other = extra_ref[k, p, c * rows : (c + 1) * rows, :].astype(jnp.float32)
        return jnp.where(flag > 0, other, summed).astype(jnp.bfloat16)

    for c in range(CHUNKS):

        @pl.loop(0, devices)
        def _(i):
            k = partner(devices - 1 - i)
            sums = [window(k, p, c) for p in range(local_pieces)]
            for p in range(local_pieces):
                pooled[k, p, c * rows : (c + 1) * rows, :] = sums[p]

            if c == 0:

                @pl.when(i == 1)
                def _():
                    pl.semaphore_wait(barrier, devices - 1)

            @pl.when(i > 0)
            def _():
                there(c, devices - i).start()

        arrived[c][me] = pooled[me, :, c * rows : (c + 1) * rows, :]

    step = next(n for n in (3 * width, width) if wide % n == 0)
    parts = [slice(i, i + step) for i in range(0, wide, step)]
    out_weight = out_w_ref[...].astype(jnp.float32)[None, :]
    row_at = lax.broadcasted_iota(jnp.int32, (rows, 2 * half), 0)
    column_at = lax.broadcasted_iota(jnp.int32, (rows, 2 * half), 1)

    for c in range(CHUNKS):
        feats[:, :width] = dense_ref[pl.ds(pl.multiple_of(role * half + c * rows, rows), rows), :].astype(jnp.float32)

        @pl.loop(1, devices)
        def _(s):
            there(c, s).wait_recv()

        def piece(index):
            return arrived[c][index // local_pieces, index % local_pieces].astype(jnp.float32)

        @pl.loop(0, tables)
        def _(t):
            def add(e, acc):
                own = plan_ref[tables + spares + e] == t
                return acc + piece(plan_ref[tables + e]) * jnp.where(own, 1.0, 0.0)

            acc = piece(plan_ref[t])
            if spares <= 16:
                for e in range(spares):
                    acc = add(e, acc)
            else:
                acc = lax.fori_loop(0, spares, add, acc)
            feats[:, pl.ds(pl.multiple_of((t + 1) * width, width), width)] = acc

        if c == 0:
            load_u.wait()
        low_rank = dot(feats[...].astype(jnp.bfloat16), u_ref[...]).astype(jnp.bfloat16)
        if c == 0:
            load_v.wait()
            load_w.wait()
        pre_act = b1_ref[...][None, :]
        for part in parts:
            cross_out = dot(low_rank, v_ref[:, part]) + bias_ref[part][None, :]
            crossed[:, part] = cross_out
            own = feats[:, part]
            pre_act = pre_act + dot((own * cross_out + own).astype(jnp.bfloat16), w_ref[part, :])
        sig_act = jax.nn.sigmoid(pre_act)
        logits = jnp.sum(pre_act * sig_act * out_weight, axis=1, keepdims=True)
        labels = jnp.sum(
            jnp.where(row_at + (role * half + c * rows) == column_at, label_ref[...][None, :], 0.0),
            axis=1,
            keepdims=True,
        )
        grad_logit = jax.nn.sigmoid(logits) - labels
        slope = sig_act * (1.0 + pre_act * (1.0 - sig_act))
        grad_act = (grad_logit * out_weight * slope).astype(jnp.bfloat16)
        grad_low = jnp.zeros((rows, u_ref.shape[1]), jnp.float32)
        for part in parts:
            grad_mixed = dot(grad_act, w_ref[part, :], NT)
            grad_cross = (grad_mixed * feats[:, part]).astype(jnp.bfloat16)
            mixed_grad[:, part] = grad_mixed * (crossed[:, part] + 1.0)
            grad_low = grad_low + dot(grad_cross, v_ref[:, part], NT)
        grad_low = grad_low.astype(jnp.bfloat16)
        for part in parts:
            whole = (mixed_grad[:, part] + dot(grad_low, u_ref[part, :], NT)).astype(jnp.bfloat16)
            for i in range(step // width):
                grads[part.start // width + i] = whole[:, i * width : (i + 1) * width]

        @pl.loop(0, devices)
        def _(d):
            for i in range(local_pieces):
                outgoing[c][d, i] = grads[owner_ref[d * local_pieces + i] + 1]

        @pl.loop(1, devices)
        def _(i):
            back(c, devices - i).start()

        out_ref[me, :, c * rows : (c + 1) * rows, :] = outgoing[c][me]

    for c in range(CHUNKS):

        @pl.loop(1, devices)
        def _(s):
            there(c, s).wait_send()
            back(c, s).wait_send()
            back(c, s).wait_recv()


def local(
    table_rows, piece_table, bag_rows, bag_of, bag_weight, dense_input, labels,
    cross_u, cross_v, cross_bias, top_w1, top_b1, out_w,
):
    devices = lax.axis_size("dev")
    local_pieces, length, width = table_rows.shape
    half = dense_input.shape[0] // 2
    rows = half // CHUNKS
    wide = cross_u.shape[0]
    tables = wide // width - 1

    def tiled(array):
        return array.reshape(local_pieces, -1, LANES).transpose(1, 0, 2)

    bag_rows, bag_of, bag_weight = tiled(bag_rows), tiled(bag_of), tiled(bag_weight)
    plans, base, extra = plan(piece_table, table_rows, bag_rows, bag_of, bag_weight, half, devices, tables)
    vmem = pl.BlockSpec(memory_space=pltpu.VMEM)
    smem = pl.BlockSpec(memory_space=pltpu.SMEM)
    hbm = pl.BlockSpec(memory_space=pltpu.HBM)
    shape = (devices, local_pieces, half, width)
    block = pltpu.VMEM((devices, local_pieces, rows, width), jnp.bfloat16)
    returned = pl.pallas_call(
        step_kernel,
        out_shape=jax.ShapeDtypeStruct(shape, jnp.bfloat16),
        in_specs=[smem] * 3 + [vmem] * 5 + [hbm] * 8,
        out_specs=vmem,
        scratch_shapes=[
            pltpu.VMEM(bag_of.shape, jnp.int32),
            pltpu.VMEM(bag_rows.shape, jnp.int32),
            pltpu.VMEM(bag_weight.shape, jnp.bfloat16),
            pltpu.VMEM(bag_weight.shape, jnp.float32),
            pltpu.VMEM(table_rows.shape, jnp.bfloat16),
            pltpu.VMEM((local_pieces, length // LOW * width, LOW), jnp.bfloat16),
            pltpu.VMEM(shape, jnp.bfloat16),
            pltpu.VMEM(shape, jnp.bfloat16),
            pltpu.VMEM(cross_u.shape, jnp.bfloat16),
            pltpu.VMEM(cross_v.shape, jnp.bfloat16),
            pltpu.VMEM(top_w1.shape, jnp.bfloat16),
            pltpu.VMEM((rows, wide), jnp.float32),
            pltpu.VMEM((rows, wide), jnp.float32),
            pltpu.VMEM((rows, wide), jnp.float32),
            pltpu.VMEM((wide // width, rows, width), jnp.bfloat16),
            [block] * CHUNKS,
            [block] * CHUNKS,
            pltpu.SemaphoreType.DMA((8,)),
        ]
        + [pltpu.SemaphoreType.DMA((CHUNKS, devices))] * 4,
        compiler_params=pltpu.CompilerParams(
            vmem_limit_bytes=60 * 1024 * 1024, collective_id=0, has_side_effects=True
        ),
    )(
        plans, base, piece_table, dense_input, labels, cross_bias, top_b1, out_w,
        bag_of, bag_rows, bag_weight, table_rows, extra, cross_u, cross_v, top_w1,
    )
    return returned.transpose(0, 2, 1, 3)


def solution(mesh):
    split, whole = P("dev"), P()
    return jax.shard_map(
        local,
        mesh=mesh,
        in_specs=(split, whole, split, split, split, split, split) + (whole,) * 6,
        out_specs=P(None, "role", "dev", None),
        check_vma=False,
    )
```

time: 93.5 us -> 76.4 us (0.82); the launches traced: 94.8 us -> 76.1 us
  Pallas kernels: 83.4 us -> 72.8 us
  local copies, waits for them, and re-layouts: 10.2 us -> 3.28 us
  other arithmetic: 1.26 us -> 0 us
    pallas_call x2, Pallas kernels: 83.4 us -> 72.8 us  [the longest x1 70.1 us: local(): pl.pallas_call(step_kernel, out_shape=jax.ShapeDtypeStruct(shape, jnp.bfl...]
    unnamed x18 -> x0, local copies, waits for them, and re-layouts: 6.9 us -> none
    reduce_sum x1 -> x0, other arithmetic: 1.25 us -> none  [pool(): jnp.sum((bag_of[:, None, :] < edges[None, :, None] + half).astype(jnp.int...]
where the time goes in v1:
time: 76.4 us; the launch traced here: 76.1 us
  Pallas kernels  72.8 us (95%)
  local copies, waits for them, and re-layouts  3.28 us (4%)
    pallas_call x1, Pallas kernels, local(): pl.pallas_call(step_kernel, out_shape=jax.ShapeDtypeStruct(shape, jnp.bfl...  70.1 us
    transpose x1, local copies, waits for them, and re-layouts, local(): return returned.transpose(0, 2, 1, 3)  3.28 us
    pallas_call x1, Pallas kernels, plan(): pl.pallas_call(functools.partial(plan_kernel, tables), out_shape=[jax.Sha...  2.79 us

profile of v1, /device:TPU:0, one launch (start us, length us, event | category | flops | bytes accessed | tf_op | source)
XLA Modules:
  0.0 76.1 jit_solution(3002263652077876095)
XLA Ops:
  0.0 2.8 %shard_map.127 = (s32[102]{0:T(128)}, s32[2,128]{1,0:T(2,128)}, bf16[16,2,128,128]{3,2,1,0:T(8,128)(2,1)}) custom-call(s32[32]{0:T(128)} %owner_ref.3, s32[64,2,128]{2,1,0:T(2,128)} %bitcast.11, s32[64,2,128]{2,1,0:T(2,128)} %bitcast.13, bf16[64,2,128]{2,1,0:T(2,128)(2,1)} %bitcast.15, bf16[2,2048,128]{2,1,0:T(8,128)(2,1)} %table_hbm.3), custom_call_target="tpu_custom_call" | custom-call | tf_op jit(solution)/shard_map/pallas_call | solution.py:153
  2.8 70.1 %shard_map.128 = bf16[16,2,128,128]{3,2,1,0:T(8,128)(2,1)} custom-call(s32[102]{0:T(128)} %get-tuple-element.8.plan_ref, s32[2,128]{1,0:T(2,128)} %get-tuple-element.9.base_ref, s32[32]{0:T(128)} %owner_ref.3, bf16[256,128]{1,0:T(8,128)(2,1)} %dense_ref.1, f32[256]{0:T(256)} %label_ref.1, f32[3456]{0:T(1024)} %bias_ref.1, f32[1024]{0:T(1024)} %b1_ref.1, ...), custom_call_target="tpu_custom_call" | custom-call | tf_op jit(solution)/shard_map/pallas_call | solution.py:398
  72.9 3.3 %copy.14 = bf16[16,128,2,128]{3,2,1,0:T(2,128)(2,1)} copy(bf16[16,128,2,128]{3,1,2,0:T(8,128)(2,1)} %bitcast.10) | data formatting | bytes 2097152 | tf_op jit(solution)/shard_map/transpose | solution.py:431

commit v2 on v1

--- a/solution.py
+++ b/solution.py
@@ -10,7 +10,8 @@
 LANES = 128
 WINDOW = 2 * LANES
 LOW = 256
-CHUNKS = 2
+HALVES = 2
+TOGETHER = 2
 NT = (((1,), (1,)), ((), ()))
 NN = (((1,), (0,)), ((), ()))
 
@@ -44,7 +45,7 @@
 ):
     blocks, pieces, half, width = extra_hbm.shape
     tiles = bags_ref.shape[0]
-    rows = half // CHUNKS
+    rows = half // HALVES
     shift = rows.bit_length() - 1
     spares = max(1, owner_ref.shape[0] - tables)
     flags = tables + 2 * spares
@@ -81,7 +82,7 @@
         plan_ref[flags + i] = 0
 
     group = lax.broadcasted_iota(jnp.int32, base_ref.shape, 1)
-    edges = (2 * (group // CHUNKS) + role) * half + group % CHUNKS * rows
+    edges = (2 * (group // HALVES) + role) * half + group % HALVES * rows
 
     ahead = WINDOW // LANES
 
@@ -116,9 +117,9 @@
 
         for p in range(pieces):
 
-            @pl.loop(0, blocks * CHUNKS)
+            @pl.loop(0, blocks * HALVES)
             def _(e):
-                k, c = e // CHUNKS, e % CHUNKS
+                k, c = e // HALVES, e % HALVES
                 edge = (2 * k + role) * half + c * rows
                 bags = bags_ref[:, p, :]
                 first = jnp.sum(jnp.where(bags < edge, 1, 0))
@@ -132,7 +133,7 @@
 
                 @pl.when(last - first > WINDOW)
                 def _():
-                    plan_ref[flags + (k * pieces + p) * CHUNKS + c] = 1
+                    plan_ref[flags + (k * pieces + p) * HALVES + c] = 1
                     end = (last + LANES - 1) // LANES
                     acc = lax.fori_loop(begin, end, more, jnp.zeros((rows, width), jnp.float32))
                     stage[...] = acc.astype(jnp.bfloat16)
@@ -146,14 +147,14 @@
 def plan(piece_table, table_rows, bag_rows, bag_of, bag_weight, half, blocks, tables):
     pieces, length, width = table_rows.shape
     spares = max(1, piece_table.shape[0] - tables)
-    lanes = -(-blocks * CHUNKS // LANES) * LANES
+    lanes = -(-blocks * HALVES // LANES) * LANES
     vmem = pl.BlockSpec(memory_space=pltpu.VMEM)
     smem = pl.BlockSpec(memory_space=pltpu.SMEM)
     hbm = pl.BlockSpec(memory_space=pltpu.HBM)
     return pl.pallas_call(
         functools.partial(plan_kernel, tables),
         out_shape=[
-            jax.ShapeDtypeStruct((tables + 2 * spares + blocks * pieces * CHUNKS,), jnp.int32),
+            jax.ShapeDtypeStruct((tables + 2 * spares + blocks * pieces * HALVES,), jnp.int32),
             jax.ShapeDtypeStruct((pieces, lanes), jnp.int32),
             jax.ShapeDtypeStruct((blocks, pieces, half, width), jnp.bfloat16),
         ],
@@ -165,7 +166,7 @@
             pltpu.VMEM(bag_weight.shape, jnp.float32),
             pltpu.VMEM(table_rows.shape, jnp.bfloat16),
             pltpu.VMEM((pieces, length // LOW * width, LOW), jnp.bfloat16),
-            pltpu.VMEM((half // CHUNKS, width), jnp.bfloat16),
+            pltpu.VMEM((half // HALVES, width), jnp.bfloat16),
             pltpu.SemaphoreType.DMA((3,)),
         ],
         compiler_params=pltpu.CompilerParams(vmem_limit_bytes=60 * 1024 * 1024),
@@ -182,6 +183,7 @@
     devices, local_pieces, half, width = out_ref.shape
     pieces = devices * local_pieces
     rows, wide = feats.shape
+    group = half // HALVES
     tables = wide // width - 1
     spares = max(1, pieces - tables)
     flags = tables + 2 * spares
@@ -221,24 +223,24 @@
             peer = peer + bit * ((me // bit + s // bit) % 2)
         return peer
 
-    def there(c, s):
+    def there(s):
         peer = partner(s)
         return pltpu.make_async_remote_copy(
-            src_ref=pooled.at[peer, :, c * rows : (c + 1) * rows, :],
-            dst_ref=arrived[c].at[me],
-            send_sem=there_send.at[c, s],
-            recv_sem=there_recv.at[c, s],
+            src_ref=pooled.at[peer],
+            dst_ref=arrived.at[me],
+            send_sem=there_send.at[s],
+            recv_sem=there_recv.at[s],
             device_id={"dev": peer},
             device_id_type=pl.DeviceIdType.MESH,
         )
 
-    def back(c, s):
+    def back(s):
         peer = partner(s)
         return pltpu.make_async_remote_copy(
-            src_ref=outgoing[c].at[peer],
-            dst_ref=out_ref.at[me, :, c * rows : (c + 1) * rows, :],
-            send_sem=back_send.at[c, s],
-            recv_sem=back_recv.at[c, s],
+            src_ref=outgoing.at[peer],
+            dst_ref=out_ref.at[me],
+            send_sem=back_send.at[s],
+            recv_sem=back_recv.at[s],
             device_id={"dev": peer},
             device_id_type=pl.DeviceIdType.MESH,
         )
@@ -250,45 +252,59 @@
         for g in range(table_ref.shape[1] // LOW):
             flipped[p, g * width : (g + 1) * width, :] = flip(table_ref[p, g * LOW : (g + 1) * LOW, :])
 
-    def window(k, p, c):
-        edge = (2 * k + role) * half + c * rows
-        at = base_ref[p, k * CHUNKS + c]
-
-        def tiles(ref):
-            return [ref[at + j, p : p + 1, :] for j in range(WINDOW // LANES + 1)]
-
-        bags = tiles(bags_ref)
-        early = bags[0] < edge
-
-        def lay(parts):
-            return jnp.concatenate([jnp.where(early, parts[-1], parts[0])] + parts[1:-1], axis=1)
-
-        picked = pick(flipped[p], width, lay(tiles(rows_ref)))
-        summed = dot(spread_out(lay(bags) - edge, lay(tiles(scale_wide)), rows), picked, NT)
-        flag = jnp.zeros((rows, width), jnp.int32) + plan_ref[flags + (k * local_pieces + p) * CHUNKS + c]
-        other = extra_ref[k, p, c * rows : (c + 1) * rows, :].astype(jnp.float32)
-        return jnp.where(flag > 0, other, summed).astype(jnp.bfloat16)
-
-    for c in range(CHUNKS):
-
-        @pl.loop(0, devices)
-        def _(i):
-            k = partner(devices - 1 - i)
-            sums = [window(k, p, c) for p in range(local_pieces)]
-            for p in range(local_pieces):
-                pooled[k, p, c * rows : (c + 1) * rows, :] = sums[p]
-
-            if c == 0:
-
-                @pl.when(i == 1)
-                def _():
-                    pl.semaphore_wait(barrier, devices - 1)
-
-            @pl.when(i > 0)
+    def windows(places, p):
+        laid = []
+        for k, c in places:
+            edge = (2 * k + role) * half + c * group
+            at = base_ref[p, k * HALVES + c]
+
+            def tiles(ref):
+                return [ref[at + j, p : p + 1, :] for j in range(WINDOW // LANES + 1)]
+
+            bags = tiles(bags_ref)
+            early = bags[0] < edge
+
+            def lay(tiles):
+                return [jnp.where(early, tiles[-1], tiles[0])] + tiles[1:-1]
+
+            laid.append((lay(tiles(rows_ref)), [bag - edge for bag in lay(bags)], lay(tiles(scale_wide))))
+        picked = pick(flipped[p], width, jnp.concatenate([tile for ids, _, _ in laid for tile in ids], axis=1))
+        sums = []
+        for n, (k, c) in enumerate(places):
+            bags, scale = (jnp.concatenate(tiles, axis=1) for tiles in laid[n][1:])
+            summed = dot(spread_out(bags, scale, group), picked[:, n * WINDOW : (n + 1) * WINDOW], NT)
+            flag = jnp.zeros((group, width), jnp.int32) + plan_ref[flags + (k * local_pieces + p) * HALVES + c]
+            other = extra_ref[k, p, c * group : (c + 1) * group, :].astype(jnp.float32)
+            sums.append(jnp.where(flag > 0, other, summed).astype(jnp.bfloat16))
+        return sums
+
+    together = TOGETHER if devices % TOGETHER == 0 else 1
+
+    def send(i):
+        for n in range(together):
+            s = devices - 1 - (i * together + n)
+
+            @pl.when(s > 0)
             def _():
-                there(c, devices - i).start()
-
-        arrived[c][me] = pooled[me, :, c * rows : (c + 1) * rows, :]
+                there(s).start()
+
+    @pl.loop(0, devices // together)
+    def _(i):
+        @pl.when(i == 1)
+        def _():
+            pl.semaphore_wait(barrier, devices - 1)
+
+        @pl.when(i > 0)
+        def _():
+            send(i - 1)
+
+        places = [(partner(devices - 1 - (i * together + n)), c) for n in range(together) for c in range(HALVES)]
+        for p in range(local_pieces):
+            for (k, c), summed in zip(places, windows(places, p)):
+                pooled[k, p, c * group : (c + 1) * group, :] = summed
+
+    arrived[me] = pooled[me]
+    send(devices // together - 1)
 
     step = next(n for n in (3 * width, width) if wide % n == 0)
     parts = [slice(i, i + step) for i in range(0, wide, step)]
@@ -296,82 +312,78 @@
     row_at = lax.broadcasted_iota(jnp.int32, (rows, 2 * half), 0)
     column_at = lax.broadcasted_iota(jnp.int32, (rows, 2 * half), 1)
 
-    for c in range(CHUNKS):
-        feats[:, :width] = dense_ref[pl.ds(pl.multiple_of(role * half + c * rows, rows), rows), :].astype(jnp.float32)
-
-        @pl.loop(1, devices)
-        def _(s):
-            there(c, s).wait_recv()
-
-        def piece(index):
-            return arrived[c][index // local_pieces, index % local_pieces].astype(jnp.float32)
-
-        @pl.loop(0, tables)
-        def _(t):
-            def add(e, acc):
-                own = plan_ref[tables + spares + e] == t
-                return acc + piece(plan_ref[tables + e]) * jnp.where(own, 1.0, 0.0)
-
-            acc = piece(plan_ref[t])
-            if spares <= 16:
-                for e in range(spares):
-                    acc = add(e, acc)
-            else:
-                acc = lax.fori_loop(0, spares, add, acc)
-            feats[:, pl.ds(pl.multiple_of((t + 1) * width, width), width)] = acc
-
-        if c == 0:
-            load_u.wait()
-        low_rank = dot(feats[...].astype(jnp.bfloat16), u_ref[...]).astype(jnp.bfloat16)
-        if c == 0:
-            load_v.wait()
-            load_w.wait()
-        pre_act = b1_ref[...][None, :]
-        for part in parts:
-            cross_out = dot(low_rank, v_ref[:, part]) + bias_ref[part][None, :]
-            crossed[:, part] = cross_out
-            own = feats[:, part]
-            pre_act = pre_act + dot((own * cross_out + own).astype(jnp.bfloat16), w_ref[part, :])
-        sig_act = jax.nn.sigmoid(pre_act)
-        logits = jnp.sum(pre_act * sig_act * out_weight, axis=1, keepdims=True)
-        labels = jnp.sum(
-            jnp.where(row_at + (role * half + c * rows) == column_at, label_ref[...][None, :], 0.0),
-            axis=1,
-            keepdims=True,
-        )
-        grad_logit = jax.nn.sigmoid(logits) - labels
-        slope = sig_act * (1.0 + pre_act * (1.0 - sig_act))
-        grad_act = (grad_logit * out_weight * slope).astype(jnp.bfloat16)
-        grad_low = jnp.zeros((rows, u_ref.shape[1]), jnp.float32)
-        for part in parts:
-            grad_mixed = dot(grad_act, w_ref[part, :], NT)
-            grad_cross = (grad_mixed * feats[:, part]).astype(jnp.bfloat16)
-            mixed_grad[:, part] = grad_mixed * (crossed[:, part] + 1.0)
-            grad_low = grad_low + dot(grad_cross, v_ref[:, part], NT)
-        grad_low = grad_low.astype(jnp.bfloat16)
-        for part in parts:
-            whole = (mixed_grad[:, part] + dot(grad_low, u_ref[part, :], NT)).astype(jnp.bfloat16)
-            for i in range(step // width):
-                grads[part.start // width + i] = whole[:, i * width : (i + 1) * width]
-
-        @pl.loop(0, devices)
-        def _(d):
-            for i in range(local_pieces):
-                outgoing[c][d, i] = grads[owner_ref[d * local_pieces + i] + 1]
-
-        @pl.loop(1, devices)
-        def _(i):
-            back(c, devices - i).start()
-
-        out_ref[me, :, c * rows : (c + 1) * rows, :] = outgoing[c][me]
-
-    for c in range(CHUNKS):
-
-        @pl.loop(1, devices)
-        def _(s):
-            there(c, s).wait_send()
-            back(c, s).wait_send()
-            back(c, s).wait_recv()
+    feats[:, :width] = dense_ref[pl.ds(pl.multiple_of(role * half, half), half), :].astype(jnp.float32)
+
+    @pl.loop(1, devices)
+    def _(s):
+        there(s).wait_recv()
+
+    def piece(index):
+        return arrived[index // local_pieces, index % local_pieces].astype(jnp.float32)
+
+    @pl.loop(0, tables)
+    def _(t):
+        def add(e, acc):
+            own = plan_ref[tables + spares + e] == t
+            return acc + piece(plan_ref[tables + e]) * jnp.where(own, 1.0, 0.0)
+
+        acc = piece(plan_ref[t])
+        if spares <= 16:
+            for e in range(spares):
+                acc = add(e, acc)
+        else:
+            acc = lax.fori_loop(0, spares, add, acc)
+        feats[:, pl.ds(pl.multiple_of((t + 1) * width, width), width)] = acc
+
+    load_u.wait()
+    low_rank = dot(feats[...].astype(jnp.bfloat16), u_ref[...]).astype(jnp.bfloat16)
+    load_v.wait()
+    load_w.wait()
+    pre_act = b1_ref[...][None, :]
+    for part in parts:
+        cross_out = dot(low_rank, v_ref[:, part]) + bias_ref[part][None, :]
+        crossed[:, part] = cross_out
+        own = feats[:, part]
+        pre_act = pre_act + dot((own * cross_out + own).astype(jnp.bfloat16), w_ref[part, :])
+    sig_act = jax.nn.sigmoid(pre_act)
+    logits = jnp.sum(pre_act * sig_act * out_weight, axis=1, keepdims=True)
+    labels = jnp.sum(
+        jnp.where(row_at + (role * half) == column_at, label_ref[...][None, :], 0.0),
+        axis=1,
+        keepdims=True,
+    )
+    grad_logit = jax.nn.sigmoid(logits) - labels
+    slope = sig_act * (1.0 + pre_act * (1.0 - sig_act))
+    grad_act = (grad_logit * out_weight * slope).astype(jnp.bfloat16)
+    grad_low = jnp.zeros((rows, u_ref.shape[1]), jnp.float32)
+    for part in parts:
+        grad_mixed = dot(grad_act, w_ref[part, :], NT)
+        grad_cross = (grad_mixed * feats[:, part]).astype(jnp.bfloat16)
+        mixed_grad[:, part] = grad_mixed * (crossed[:, part] + 1.0)
+        grad_low = grad_low + dot(grad_cross, v_ref[:, part], NT)
+    grad_low = grad_low.astype(jnp.bfloat16)
+    for part in parts:
+        whole = (mixed_grad[:, part] + dot(grad_low, u_ref[part, :], NT)).astype(jnp.bfloat16)
+        for i in range(step // width):
+            grads[part.start // width + i] = whole[:, i * width : (i + 1) * width]
+
+    @pl.loop(0, devices)
+    def _(i):
+        d = partner(devices - 1 - i)
+        for p in range(local_pieces):
+            outgoing[d, p] = grads[owner_ref[d * local_pieces + p] + 1]
+
+        @pl.when(i > 0)
+        def _():
+            back(devices - i).start()
+
+    out_ref[me] = outgoing[me]
+
+    @pl.loop(1, devices)
+    def _(s):
+        there(s).wait_send()
+        back(s).wait_send()
+        back(s).wait_recv()
 
 
 def local(
@@ -381,7 +393,6 @@
     devices = lax.axis_size("dev")
     local_pieces, length, width = table_rows.shape
     half = dense_input.shape[0] // 2
-    rows = half // CHUNKS
     wide = cross_u.shape[0]
     tables = wide // width - 1
 
@@ -394,7 +405,6 @@
     smem = pl.BlockSpec(memory_space=pltpu.SMEM)
     hbm = pl.BlockSpec(memory_space=pltpu.HBM)
     shape = (devices, local_pieces, half, width)
-    block = pltpu.VMEM((devices, local_pieces, rows, width), jnp.bfloat16)
     returned = pl.pallas_call(
         step_kernel,
         out_shape=jax.ShapeDtypeStruct(shape, jnp.bfloat16),
@@ -412,15 +422,15 @@
             pltpu.VMEM(cross_u.shape, jnp.bfloat16),
             pltpu.VMEM(cross_v.shape, jnp.bfloat16),
             pltpu.VMEM(top_w1.shape, jnp.bfloat16),
-            pltpu.VMEM((rows, wide), jnp.float32),
-            pltpu.VMEM((rows, wide), jnp.float32),
-            pltpu.VMEM((rows, wide), jnp.float32),
-            pltpu.VMEM((wide // width, rows, width), jnp.bfloat16),
-            [block] * CHUNKS,
-            [block] * CHUNKS,
+            pltpu.VMEM((half, wide), jnp.float32),
+            pltpu.VMEM((half, wide), jnp.float32),
+            pltpu.VMEM((half, wide), jnp.float32),
+            pltpu.VMEM((wide // width, half, width), jnp.bfloat16),
+            pltpu.VMEM(shape, jnp.bfloat16),
+            pltpu.VMEM(shape, jnp.bfloat16),
             pltpu.SemaphoreType.DMA((8,)),
         ]
-        + [pltpu.SemaphoreType.DMA((CHUNKS, devices))] * 4,
+        + [pltpu.SemaphoreType.DMA((devices,))] * 4,
         compiler_params=pltpu.CompilerParams(
             vmem_limit_bytes=60 * 1024 * 1024, collective_id=0, has_side_effects=True
         ),

time: 76.4 us -> 72.6 us (0.950)
  Pallas kernels: 72.8 us -> 69.1 us
    pallas_call x1, Pallas kernels: 70.1 us -> 66.3 us  [local(): pl.pallas_call(step_kernel, out_shape=jax.ShapeDtypeStruct(shape, jnp.bfl...]
where the time goes in v2:
time: 72.6 us; the launch traced here: 72.4 us
  Pallas kernels  69.1 us (95%)
  local copies, waits for them, and re-layouts  3.28 us (5%)
    pallas_call x1, Pallas kernels, local(): pl.pallas_call(step_kernel, out_shape=jax.ShapeDtypeStruct(shape, jnp.bfl...  66.3 us
    transpose x1, local copies, waits for them, and re-layouts, local(): return returned.transpose(0, 2, 1, 3)  3.28 us
    pallas_call x1, Pallas kernels, plan(): pl.pallas_call(functools.partial(plan_kernel, tables), out_shape=[jax.Sha...  2.79 us

profile of v2, /device:TPU:0, one launch (start us, length us, event | category | flops | bytes accessed | tf_op | source)
XLA Modules:
  0.0 72.4 jit_solution(13500661681930156824)
XLA Ops:
  0.0 2.8 %shard_map.127 = (s32[102]{0:T(128)}, s32[2,128]{1,0:T(2,128)}, bf16[16,2,128,128]{3,2,1,0:T(8,128)(2,1)}) custom-call(s32[32]{0:T(128)} %owner_ref.3, s32[64,2,128]{2,1,0:T(2,128)} %bitcast.11, s32[64,2,128]{2,1,0:T(2,128)} %bitcast.13, bf16[64,2,128]{2,1,0:T(2,128)(2,1)} %bitcast.15, bf16[2,2048,128]{2,1,0:T(8,128)(2,1)} %table_hbm.3), custom_call_target="tpu_custom_call" | custom-call | tf_op jit(solution)/shard_map/pallas_call | solution.py:154
  2.8 66.3 %shard_map.128 = bf16[16,2,128,128]{3,2,1,0:T(8,128)(2,1)} custom-call(s32[102]{0:T(128)} %get-tuple-element.8.plan_ref, s32[2,128]{1,0:T(2,128)} %get-tuple-element.9.base_ref, s32[32]{0:T(128)} %owner_ref.3, bf16[256,128]{1,0:T(8,128)(2,1)} %dense_ref.1, f32[256]{0:T(256)} %label_ref.1, f32[3456]{0:T(1024)} %bias_ref.1, f32[1024]{0:T(1024)} %b1_ref.1, ...), custom_call_target="tpu_custom_call" | custom-call | tf_op jit(solution)/shard_map/pallas_call | solution.py:408
  69.1 3.3 %copy.14 = bf16[16,128,2,128]{3,2,1,0:T(2,128)(2,1)} copy(bf16[16,128,2,128]{3,1,2,0:T(8,128)(2,1)} %bitcast.10) | data formatting | bytes 2097152 | tf_op jit(solution)/shard_map/transpose | solution.py:441

commit v3 on v1

--- a/solution.py
+++ b/solution.py
@@ -11,6 +11,7 @@
 WINDOW = 2 * LANES
 LOW = 256
 CHUNKS = 2
+TOGETHER = 4
 NT = (((1,), (1,)), ((), ()))
 NN = (((1,), (0,)), ((), ()))
 
@@ -39,8 +40,8 @@
 
 
 def plan_kernel(
-    tables, owner_ref, bags_ref, rows_hbm, scale_hbm, table_hbm, plan_ref, base_ref, extra_hbm,
-    rows_ref, scale_ref, scale_wide, table_ref, flipped, stage, sems,
+    tables, owner_ref, bags_hbm, rows_hbm, scale_hbm, table_hbm, plan_ref, base_ref, extra_hbm,
+    bags_ref, rows_ref, scale_ref, scale_wide, table_ref, flipped, stage, sems,
 ):
     blocks, pieces, half, width = extra_hbm.shape
     tiles = bags_ref.shape[0]
@@ -48,7 +49,10 @@
     shift = rows.bit_length() - 1
     spares = max(1, owner_ref.shape[0] - tables)
     flags = tables + 2 * spares
+    owners = flags + blocks * pieces * CHUNKS
     role = lax.axis_index("role")
+    load_bags = pltpu.make_async_copy(bags_hbm, bags_ref, sems.at[3])
+    load_bags.start()
 
     @pl.loop(0, tables)
     def _(t):
@@ -61,6 +65,7 @@
 
     def assign(p, used):
         t = owner_ref[p]
+        plan_ref[owners + p] = t
         again = plan_ref[t] >= 0
 
         @pl.when(again)
@@ -76,9 +81,11 @@
 
     lax.fori_loop(0, owner_ref.shape[0], assign, jnp.int32(0))
 
-    @pl.loop(0, plan_ref.shape[0] - flags)
+    @pl.loop(0, owners - flags)
     def _(i):
         plan_ref[flags + i] = 0
+
+    load_bags.wait()
 
     group = lax.broadcasted_iota(jnp.int32, base_ref.shape, 1)
     edges = (2 * (group // CHUNKS) + role) * half + group % CHUNKS * rows
@@ -147,34 +154,36 @@
     pieces, length, width = table_rows.shape
     spares = max(1, piece_table.shape[0] - tables)
     lanes = -(-blocks * CHUNKS // LANES) * LANES
+    entries = tables + 2 * spares + blocks * pieces * CHUNKS + piece_table.shape[0]
     vmem = pl.BlockSpec(memory_space=pltpu.VMEM)
     smem = pl.BlockSpec(memory_space=pltpu.SMEM)
     hbm = pl.BlockSpec(memory_space=pltpu.HBM)
     return pl.pallas_call(
         functools.partial(plan_kernel, tables),
         out_shape=[
-            jax.ShapeDtypeStruct((tables + 2 * spares + blocks * pieces * CHUNKS,), jnp.int32),
+            jax.ShapeDtypeStruct((-(-entries // LANES) * LANES,), jnp.int32),
             jax.ShapeDtypeStruct((pieces, lanes), jnp.int32),
             jax.ShapeDtypeStruct((blocks, pieces, half, width), jnp.bfloat16),
         ],
-        in_specs=[smem, vmem, hbm, hbm, hbm],
+        in_specs=[smem, hbm, hbm, hbm, hbm],
         out_specs=[smem, vmem, hbm],
         scratch_shapes=[
+            pltpu.VMEM(bag_of.shape, jnp.int32),
             pltpu.VMEM(bag_rows.shape, jnp.int32),
             pltpu.VMEM(bag_weight.shape, jnp.bfloat16),
             pltpu.VMEM(bag_weight.shape, jnp.float32),
             pltpu.VMEM(table_rows.shape, jnp.bfloat16),
             pltpu.VMEM((pieces, length // LOW * width, LOW), jnp.bfloat16),
             pltpu.VMEM((half // CHUNKS, width), jnp.bfloat16),
-            pltpu.SemaphoreType.DMA((3,)),
+            pltpu.SemaphoreType.DMA((4,)),
         ],
         compiler_params=pltpu.CompilerParams(vmem_limit_bytes=60 * 1024 * 1024),
     )(piece_table, bag_of, bag_rows, bag_weight, table_rows)
 
 
 def step_kernel(
-    plan_ref, base_ref, owner_ref, dense_ref, label_ref, bias_ref, b1_ref, out_w_ref,
-    bags_hbm, rows_hbm, scale_hbm, table_hbm, extra_hbm, u_hbm, v_hbm, w_hbm, out_ref,
+    plan_hbm, base_hbm, dense_hbm, label_hbm, bias_hbm, b1_hbm, out_w_hbm, bags_hbm, rows_hbm, scale_hbm, table_hbm, extra_hbm, u_hbm, v_hbm, w_hbm, out_ref,
+    plan_ref, base_ref, dense_ref, label_ref, bias_ref, b1_ref, out_w_ref,
     bags_ref, rows_ref, scale_ref, scale_wide, table_ref, flipped, extra_ref, pooled,
     u_ref, v_ref, w_ref, feats, crossed, mixed_grad, grads, arrived, outgoing,
     sems, there_send, there_recv, back_send, back_recv,
@@ -185,21 +194,23 @@
     tables = wide // width - 1
     spares = max(1, pieces - tables)
     flags = tables + 2 * spares
+    owners = flags + devices * local_pieces * CHUNKS
     role = lax.axis_index("role")
     me = lax.axis_index("dev")
-    small = [
-        pltpu.make_async_copy(bags_hbm, bags_ref, sems.at[0]),
-        pltpu.make_async_copy(rows_hbm, rows_ref, sems.at[1]),
-        pltpu.make_async_copy(scale_hbm, scale_ref, sems.at[2]),
-        pltpu.make_async_copy(table_hbm, table_ref, sems.at[3]),
-        pltpu.make_async_copy(extra_hbm, extra_ref, sems.at[4]),
+    first = [
+        (table_hbm, table_ref), (scale_hbm, scale_ref), (bags_hbm, bags_ref), (rows_hbm, rows_ref),
+        (plan_hbm, plan_ref), (base_hbm, base_ref), (extra_hbm, extra_ref),
     ]
-    load_u = pltpu.make_async_copy(u_hbm, u_ref, sems.at[5])
-    load_v = pltpu.make_async_copy(v_hbm, v_ref, sems.at[6])
-    load_w = pltpu.make_async_copy(w_hbm, w_ref, sems.at[7])
+    later = [
+        (dense_hbm, dense_ref), (label_hbm, label_ref), (bias_hbm, bias_ref), (b1_hbm, b1_ref), (out_w_hbm, out_w_ref),
+    ]
+    loads = [pltpu.make_async_copy(*pair, sems.at[3 + n]) for n, pair in enumerate(first + later)]
+    load_u = pltpu.make_async_copy(u_hbm, u_ref, sems.at[0])
+    load_v = pltpu.make_async_copy(v_hbm, v_ref, sems.at[1])
+    load_w = pltpu.make_async_copy(w_hbm, w_ref, sems.at[2])
     barrier = pltpu.get_barrier_semaphore()
 
-    for load in small:
+    for load in loads:
         load.start()
 
     @pl.loop(1, devices)
@@ -243,41 +254,57 @@
             device_id_type=pl.DeviceIdType.MESH,
         )
 
-    for load in small:
-        load.wait()
-    scale_wide[...] = scale_ref[...].astype(jnp.float32)
+    loads[0].wait()
     for p in range(local_pieces):
         for g in range(table_ref.shape[1] // LOW):
             flipped[p, g * width : (g + 1) * width, :] = flip(table_ref[p, g * LOW : (g + 1) * LOW, :])
-
-    def window(k, p, c):
-        edge = (2 * k + role) * half + c * rows
-        at = base_ref[p, k * CHUNKS + c]
-
-        def tiles(ref):
-            return [ref[at + j, p : p + 1, :] for j in range(WINDOW // LANES + 1)]
-
-        bags = tiles(bags_ref)
-        early = bags[0] < edge
-
-        def lay(parts):
-            return jnp.concatenate([jnp.where(early, parts[-1], parts[0])] + parts[1:-1], axis=1)
-
-        picked = pick(flipped[p], width, lay(tiles(rows_ref)))
-        summed = dot(spread_out(lay(bags) - edge, lay(tiles(scale_wide)), rows), picked, NT)
-        flag = jnp.zeros((rows, width), jnp.int32) + plan_ref[flags + (k * local_pieces + p) * CHUNKS + c]
-        other = extra_ref[k, p, c * rows : (c + 1) * rows, :].astype(jnp.float32)
-        return jnp.where(flag > 0, other, summed).astype(jnp.bfloat16)
+    for load in loads[1 : len(first)]:
+        load.wait()
+    scale_wide[...] = scale_ref[...].astype(jnp.float32)
+
+    def windows(places, p):
+        laid = []
+        for k, c in places:
+            edge = (2 * k + role) * half + c * rows
+            at = base_ref[p, k * CHUNKS + c]
+
+            def tiles(ref):
+                return [ref[at + j, p : p + 1, :] for j in range(WINDOW // LANES + 1)]
+
+            bags = tiles(bags_ref)
+            early = bags[0] < edge
+
+            def lay(tiles):
+                return [jnp.where(early, tiles[-1], tiles[0])] + tiles[1:-1]
+
+            laid.append((lay(tiles(rows_ref)), [bag - edge for bag in lay(bags)], lay(tiles(scale_wide))))
+        picked = pick(flipped[p], width, jnp.concatenate([tile for ids, _, _ in laid for tile in ids], axis=1))
+        sums = []
+        for n, (k, c) in enumerate(places):
+            bags, scale = (jnp.concatenate(tiles, axis=1) for tiles in laid[n][1:])
+            summed = dot(spread_out(bags, scale, rows), picked[:, n * WINDOW : (n + 1) * WINDOW], NT)
+            flag = jnp.zeros((rows, width), jnp.int32) + plan_ref[flags + (k * local_pieces + p) * CHUNKS + c]
+            other = extra_ref[k, p, c * rows : (c + 1) * rows, :].astype(jnp.float32)
+            sums.append(jnp.where(flag > 0, other, summed).astype(jnp.bfloat16))
+        return sums
+
+    together = TOGETHER if devices % TOGETHER == 0 else 1
+
+    def turn(i):
+        return devices - 1 - i
+
+    def send(c, i):
+        for n in range(together):
+            s = turn(i * together + n)
+
+            @pl.when(s > 0)
+            def _():
+                there(c, s).start()
 
     for c in range(CHUNKS):
 
-        @pl.loop(0, devices)
+        @pl.loop(0, devices // together)
         def _(i):
-            k = partner(devices - 1 - i)
-            sums = [window(k, p, c) for p in range(local_pieces)]
-            for p in range(local_pieces):
-                pooled[k, p, c * rows : (c + 1) * rows, :] = sums[p]
-
             if c == 0:
 
                 @pl.when(i == 1)
@@ -286,12 +313,20 @@
 
             @pl.when(i > 0)
             def _():
-                there(c, devices - i).start()
+                send(c, i - 1)
+
+            places = [(partner(turn(i * together + n)), c) for n in range(together)]
+            for p in range(local_pieces):
+                for (k, _), summed in zip(places, windows(places, p)):
+                    pooled[k, p, c * rows : (c + 1) * rows, :] = summed
 
         arrived[c][me] = pooled[me, :, c * rows : (c + 1) * rows, :]
+        send(c, devices // together - 1)
 
     step = next(n for n in (3 * width, width) if wide % n == 0)
     parts = [slice(i, i + step) for i in range(0, wide, step)]
+    for load in loads[len(first) :]:
+        load.wait()
     out_weight = out_w_ref[...].astype(jnp.float32)[None, :]
     row_at = lax.broadcasted_iota(jnp.int32, (rows, 2 * half), 0)
     column_at = lax.broadcasted_iota(jnp.int32, (rows, 2 * half), 1)
@@ -355,13 +390,14 @@
                 grads[part.start // width + i] = whole[:, i * width : (i + 1) * width]
 
         @pl.loop(0, devices)
-        def _(d):
-            for i in range(local_pieces):
-                outgoing[c][d, i] = grads[owner_ref[d * local_pieces + i] + 1]
-
-        @pl.loop(1, devices)
         def _(i):
-            back(c, devices - i).start()
+            d = partner(turn(i))
+            for p in range(local_pieces):
+                outgoing[c][d, p] = grads[plan_ref[owners + d * local_pieces + p] + 1]
+
+            @pl.when(i > 0)
+            def _():
+                back(c, turn(i - 1)).start()
 
         out_ref[me, :, c * rows : (c + 1) * rows, :] = outgoing[c][me]
 
@@ -391,16 +427,22 @@
     bag_rows, bag_of, bag_weight = tiled(bag_rows), tiled(bag_of), tiled(bag_weight)
     plans, base, extra = plan(piece_table, table_rows, bag_rows, bag_of, bag_weight, half, devices, tables)
     vmem = pl.BlockSpec(memory_space=pltpu.VMEM)
-    smem = pl.BlockSpec(memory_space=pltpu.SMEM)
     hbm = pl.BlockSpec(memory_space=pltpu.HBM)
     shape = (devices, local_pieces, half, width)
     block = pltpu.VMEM((devices, local_pieces, rows, width), jnp.bfloat16)
     returned = pl.pallas_call(
         step_kernel,
         out_shape=jax.ShapeDtypeStruct(shape, jnp.bfloat16),
-        in_specs=[smem] * 3 + [vmem] * 5 + [hbm] * 8,
+        in_specs=[hbm] * 15,
         out_specs=vmem,
         scratch_shapes=[
+            pltpu.SMEM(plans.shape, jnp.int32),
+            pltpu.SMEM(base.shape, jnp.int32),
+            pltpu.VMEM(dense_input.shape, jnp.bfloat16),
+            pltpu.VMEM(labels.shape, jnp.float32),
+            pltpu.VMEM(cross_bias.shape, jnp.float32),
+            pltpu.VMEM(top_b1.shape, jnp.float32),
+            pltpu.VMEM(out_w.shape, jnp.bfloat16),
             pltpu.VMEM(bag_of.shape, jnp.int32),
             pltpu.VMEM(bag_rows.shape, jnp.int32),
             pltpu.VMEM(bag_weight.shape, jnp.bfloat16),
@@ -418,14 +460,14 @@
             pltpu.VMEM((wide // width, rows, width), jnp.bfloat16),
             [block] * CHUNKS,
             [block] * CHUNKS,
-            pltpu.SemaphoreType.DMA((8,)),
+            pltpu.SemaphoreType.DMA((15,)),
         ]
         + [pltpu.SemaphoreType.DMA((CHUNKS, devices))] * 4,
         compiler_params=pltpu.CompilerParams(
             vmem_limit_bytes=60 * 1024 * 1024, collective_id=0, has_side_effects=True
         ),
     )(
-        plans, base, piece_table, dense_input, labels, cross_bias, top_b1, out_w,
+        plans, base, dense_input, labels, cross_bias, top_b1, out_w,
         bag_of, bag_rows, bag_weight, table_rows, extra, cross_u, cross_v, top_w1,
     )
     return returned.transpose(0, 2, 1, 3)

time: 76.4 us -> 64.4 us (0.84)
  Pallas kernels: 72.8 us -> 60.6 us
    pallas_call x1, Pallas kernels: 70.1 us -> 58 us  [local(): pl.pallas_call(step_kernel, out_shape=jax.ShapeDtypeStruct(shape, jnp.bfl...]
where the time goes in v3:
time: 64.4 us; the launch traced here: 63.9 us
  Pallas kernels  60.6 us (94%)
  local copies, waits for them, and re-layouts  3.28 us (5%)
    pallas_call x1, Pallas kernels, local(): pl.pallas_call(step_kernel, out_shape=jax.ShapeDtypeStruct(shape, jnp.bfl...  58 us
    transpose x1, local copies, waits for them, and re-layouts, local(): return returned.transpose(0, 2, 1, 3)  3.28 us
    pallas_call x1, Pallas kernels, plan(): pl.pallas_call(functools.partial(plan_kernel, tables), out_shape=[jax.Sha...  2.61 us

profile of v3, /device:TPU:0, one launch (start us, length us, event | category | flops | bytes accessed | tf_op | source)
XLA Modules:
  0.0 63.9 jit_solution(9204306931287056060)
XLA Ops:
  0.0 2.6 %shard_map.127 = (s32[256]{0:T(256)}, s32[2,128]{1,0:T(2,128)}, bf16[16,2,128,128]{3,2,1,0:T(8,128)(2,1)}) custom-call(s32[32]{0:T(128)} %owner_ref.1, s32[64,2,128]{2,1,0:T(2,128)} %bitcast.11, s32[64,2,128]{2,1,0:T(2,128)} %bitcast.13, bf16[64,2,128]{2,1,0:T(2,128)(2,1)} %bitcast.15, bf16[2,2048,128]{2,1,0:T(8,128)(2,1)} %table_hbm.3), custom_call_target="tpu_custom_call" | custom-call | tf_op jit(solution)/shard_map/pallas_call | solution.py:161
  2.6 58.0 %shard_map.128 = bf16[16,2,128,128]{3,2,1,0:T(8,128)(2,1)} custom-call(s32[256]{0:T(256)} %get-tuple-element.8.plan_hbm, s32[2,128]{1,0:T(2,128)} %get-tuple-element.9.base_hbm, bf16[256,128]{1,0:T(8,128)(2,1)} %dense_hbm.1, f32[256]{0:T(256)} %label_hbm.1, f32[3456]{0:T(1024)} %bias_hbm.1, f32[1024]{0:T(1024)} %b1_hbm.1, bf16[1024]{0:T(1024)(128)(2,1)} %out_w_hbm.1, ...), custom_call_target="tpu_custom_call" | custom-call | tf_op jit(solution)/shard_map/pallas_call | solution.py:433
  60.6 3.3 %copy.14 = bf16[16,128,2,128]{3,2,1,0:T(2,128)(2,1)} copy(bf16[16,128,2,128]{3,1,2,0:T(8,128)(2,1)} %bitcast.10) | data formatting | bytes 2097152 | tf_op jit(solution)/shard_map/transpose | solution.py:473

commit v4 on v3

--- a/solution.py
+++ b/solution.py
@@ -241,6 +241,11 @@
             recv_sem=there_recv.at[c, s],
             device_id={"dev": peer},
             device_id_type=pl.DeviceIdType.MESH,
+        )
+
+    def keep(c):
+        return pltpu.make_async_copy(
+            outgoing[c].at[me], out_ref.at[me, :, c * rows : (c + 1) * rows, :], sems.at[15 + c]
         )
 
     def back(c, s):
@@ -399,9 +404,10 @@
             def _():
                 back(c, turn(i - 1)).start()
 
-        out_ref[me, :, c * rows : (c + 1) * rows, :] = outgoing[c][me]
+        keep(c).start()
 
     for c in range(CHUNKS):
+        keep(c).wait()
 
         @pl.loop(1, devices)
         def _(s):
@@ -426,7 +432,6 @@
 
     bag_rows, bag_of, bag_weight = tiled(bag_rows), tiled(bag_of), tiled(bag_weight)
     plans, base, extra = plan(piece_table, table_rows, bag_rows, bag_of, bag_weight, half, devices, tables)
-    vmem = pl.BlockSpec(memory_space=pltpu.VMEM)
     hbm = pl.BlockSpec(memory_space=pltpu.HBM)
     shape = (devices, local_pieces, half, width)
     block = pltpu.VMEM((devices, local_pieces, rows, width), jnp.bfloat16)
@@ -434,7 +439,7 @@
         step_kernel,
         out_shape=jax.ShapeDtypeStruct(shape, jnp.bfloat16),
         in_specs=[hbm] * 15,
-        out_specs=vmem,
+        out_specs=hbm,
         scratch_shapes=[
             pltpu.SMEM(plans.shape, jnp.int32),
             pltpu.SMEM(base.shape, jnp.int32),
@@ -460,7 +465,7 @@
             pltpu.VMEM((wide // width, rows, width), jnp.bfloat16),
             [block] * CHUNKS,
             [block] * CHUNKS,
-            pltpu.SemaphoreType.DMA((15,)),
+            pltpu.SemaphoreType.DMA((15 + CHUNKS,)),
         ]
         + [pltpu.SemaphoreType.DMA((CHUNKS, devices))] * 4,
         compiler_params=pltpu.CompilerParams(

time: 64.4 us -> 63.5 us (0.986)
  Pallas kernels: 60.6 us -> 59.6 us
    pallas_call x1, Pallas kernels: 58 us -> 57 us  [local(): pl.pallas_call(step_kernel, out_shape=jax.ShapeDtypeStruct(shape, jnp.bfl...]
where the time goes in v4:
time: 63.5 us; the launch traced here: 62.9 us
  Pallas kernels  59.6 us (94%)
  local copies, waits for them, and re-layouts  3.28 us (5%)
    pallas_call x1, Pallas kernels, local(): pl.pallas_call(step_kernel, out_shape=jax.ShapeDtypeStruct(shape, jnp.bfl...  57 us
    transpose x1, local copies, waits for them, and re-layouts, local(): return returned.transpose(0, 2, 1, 3)  3.28 us
    pallas_call x1, Pallas kernels, plan(): pl.pallas_call(functools.partial(plan_kernel, tables), out_shape=[jax.Sha...  2.61 us

profile of v4, /device:TPU:0, one launch (start us, length us, event | category | flops | bytes accessed | tf_op | source)
XLA Modules:
  0.0 62.9 jit_solution(4641552477324003315)
XLA Ops:
  0.0 2.6 %shard_map.127 = (s32[256]{0:T(256)}, s32[2,128]{1,0:T(2,128)}, bf16[16,2,128,128]{3,2,1,0:T(8,128)(2,1)}) custom-call(s32[32]{0:T(128)} %owner_ref.1, s32[64,2,128]{2,1,0:T(2,128)} %bitcast.11, s32[64,2,128]{2,1,0:T(2,128)} %bitcast.13, bf16[64,2,128]{2,1,0:T(2,128)(2,1)} %bitcast.15, bf16[2,2048,128]{2,1,0:T(8,128)(2,1)} %table_hbm.3), custom_call_target="tpu_custom_call" | custom-call | tf_op jit(solution)/shard_map/pallas_call | solution.py:161
  2.6 57.0 %shard_map.128 = bf16[16,2,128,128]{3,2,1,0:T(8,128)(2,1)} custom-call(s32[256]{0:T(256)} %get-tuple-element.8.plan_hbm, s32[2,128]{1,0:T(2,128)} %get-tuple-element.9.base_hbm, bf16[256,128]{1,0:T(8,128)(2,1)} %dense_hbm.1, f32[256]{0:T(256)} %label_hbm.1, f32[3456]{0:T(1024)} %bias_hbm.1, f32[1024]{0:T(1024)} %b1_hbm.1, bf16[1024]{0:T(1024)(128)(2,1)} %out_w_hbm.1, ...), custom_call_target="tpu_custom_call" | custom-call | tf_op jit(solution)/shard_map/pallas_call | solution.py:438
  59.6 3.3 %copy.14 = bf16[16,128,2,128]{3,2,1,0:T(2,128)(2,1)} copy(bf16[16,128,2,128]{3,1,2,0:T(8,128)(2,1)} %bitcast.10) | data formatting | bytes 2097152 | tf_op jit(solution)/shard_map/transpose | solution.py:478
